TPU v7x, 32 devices: a whole 2x2x4 slice. The times are simulated.
32 devices in a mesh: outer: 4 (over y, x), inner: 8 (over z, core).
Axes of the slice: x: 2, y: 2, z: 4, core: 2. Of those that a mesh axis runs over, the one named last changes fastest.
Arguments:
- tokens: bfloat16 [4096, 4096], P('inner', 'outer'), may hold values from -6 to 6
- cotangent: bfloat16 [4096, 4096], P('inner', 'outer'), may hold values from -0.09375 to 0.09375
- weight_cache: bfloat16 [4096, 4096], P(None, 'outer'), may hold values from -0.09375 to 0.09375
- weight_delta: bfloat16 [4096, 4096], P('inner', 'outer'), may hold values from -0.078125 to 0.078125
- sign_bits: int32 [4096], P('outer'), may hold values from 0 to 1
- master: float32 [4096, 4096], P('inner', 'outer'), may hold values from -1.5 to 1.5
- moment: float32 [4096, 4096], P('inner', 'outer'), may hold values from -6 to 6
- variance: float32 [4096, 4096], P('inner', 'outer'), may hold values from 0.25 to 4
Outputs:
- activation: float32 [4096, 4096], P('inner', 'outer')
- new_master: float32 [4096, 4096], P('inner', 'outer')
- new_moment: float32 [4096, 4096], P('inner', 'outer')
- new_variance: float32 [4096, 4096], P('inner', 'outer')
- block_scales: float32 [4096, 32], P('inner', 'outer')
All inputs are finite; a program needn't handle non-finite values.
Results may differ from a plain program's by a relative error of at most 0.003.
Values may be sent and summed in bfloat16 or wider, within the bound.
No kernel may reach another device: no remote copies, remote signals or barrier semaphores. Data moves between devices by JAX's collectives and lax.ppermute only.
A program may use at most 128 MiB of HBM per device.

v0:
```python
import jax
import jax.numpy as jnp
from jax import lax
from jax.sharding import PartitionSpec as P

BLOCK = 128


def hadamard_table(length):
    first = jnp.arange(length, dtype=jnp.int32)[:, None]
    second = jnp.arange(length, dtype=jnp.int32)[None, :]
    common = jnp.bitwise_and(first, second)
    parity = jnp.zeros((length, length), jnp.int32)
    for place in range(length.bit_length() - 1):
        parity = parity + jnp.bitwise_and(jnp.right_shift(common, place), 1)
    return (1 - 2 * (parity % 2)).astype(jnp.float32) / jnp.sqrt(jnp.float32(length))


def smooth(values, signs, table):
    height = values.shape[0]
    blocks = values.reshape(height, -1, table.shape[0]) * signs.reshape(-1, table.shape[0])
    mixed = jnp.einsum("rbk,kj->rbj", blocks, table, precision=lax.Precision.HIGHEST)
    return mixed.reshape(height, -1)


def unsmooth(values, signs, table):
    height = values.shape[0]
    blocks = values.reshape(height, -1, table.shape[0])
    mixed = jnp.einsum("rbj,jk->rbk", blocks, table, precision=lax.Precision.HIGHEST)
    return (mixed * signs.reshape(-1, table.shape[0])).reshape(height, -1)


def outer_product(left, right):
    return lax.dot_general(
        left, right, (((0,), (0,)), ((), ())), preferred_element_type=jnp.float32
    )


def body(tokens, cotangent, weight_cache, weight_delta, sign_bits, master, moment, variance):
    table = hadamard_table(BLOCK)
    signs = (1 - 2 * sign_bits).astype(jnp.float32)
    shard_rows = master.shape[0]
    gathered = lax.all_gather(tokens, "outer", axis=1, tiled=True)
    merged = (
        weight_cache.astype(jnp.float32)
        + lax.all_gather(weight_delta, "inner", axis=0, tiled=True).astype(jnp.float32)
    ).astype(jnp.bfloat16)
    columns = gathered
    output = jnp.dot(columns, merged, preferred_element_type=jnp.float32)
    columns = gathered
    partial_value = outer_product(columns, cotangent)
    summed = lax.psum_scatter(
        smooth(partial_value, signs, table), "inner", scatter_dimension=0, tiled=True
    )
    block_scales = jnp.max(jnp.abs(summed.reshape(shard_rows, -1, BLOCK)), axis=2)
    restored = unsmooth(summed, signs, table)
    new_moment = 0.9 * moment + 0.1 * restored
    new_variance = 0.95 * variance + 0.05 * restored * restored
    corrected = new_moment / (1.0 - 0.9**10)
    spread = jnp.sqrt(new_variance / (1.0 - 0.95**10)) + 1e-08
    new_master = master - 0.01 * (corrected / spread + 0.1 * master)
    return (output, new_master, new_moment, new_variance, block_scales)


def solution(mesh):
    placed = (
        P("inner", "outer"),
        P("inner", "outer"),
        P(None, "outer"),
        P("inner", "outer"),
        P("outer"),
        P("inner", "outer"),
        P("inner", "outer"),
        P("inner", "outer"),
    )
    return jax.shard_map(
        body,
        mesh=mesh,
        in_specs=placed,
        out_specs=(
            P("inner", "outer"),
            P("inner", "outer"),
            P("inner", "outer"),
            P("inner", "outer"),
            P("inner", "outer"),
        ),
        check_vma=False,
    )
```

profile of v0, /device:TPU:0, one launch (start us, length us, event | category | flops | bytes accessed | tf_op | source)
XLA Modules:
  0.0 339.3 jit_solution(2101183331217404971)
XLA Ops:
  7.2 0.0 copy-start
  7.2 0.0 copy-start.3
  7.2 0.0 all-gather.5.cloned.1.call-start
  7.2 0.7 all-gather.5.cloned.1.call-update
  7.9 0.0 all-gather.3.cloned.1.call-start
  8.0 0.7 all-gather.3.cloned.1.call-update
  8.7 0.0 reduce-scatter.2.cloned.1.call-start
  8.7 0.0 copy-done.3
  8.7 56.4 %all-gather.5.cloned.1.call-done = bf16[512,4096]{1,0:T(8,128)(2,1)} async-done(((bf16[512,1024]{1,0:T(8,128)(2,1)}), bf16[512,4096]{1,0:T(8,128)(2,1)}) %all-gather.5.cloned.1.call-update) | async-done | bytes 4194320 | tf_op jit(solution)/shard_map/all_gather | solution.py:43
  65.2 0.0 copy-done
  65.2 11.0 %fusion.47 = f32[4096,1024]{0,1:T(8,128)} fusion(bf16[512,4096]{1,0:T(8,128)(2,1)} %all-gather.5.cloned.1.call-done, bf16[512,1024]{1,0:T(8,128)(2,1)S(1)} %copy-done), kind=kOutput, calls=%fused_computation.54 | convolution fusion | flops 4294967296 | bytes 22020096 | tf_op jit(solution)/shard_map/dot_general | solution.py:34
  76.2 17.8 %copy.18 = f32[4096,8,128]{2,0,1:T(8,128)} copy(f32[4096,8,128]{0,2,1:T(8,128)} %bitcast.18) | data formatting | bytes 33554432 | tf_op jit(solution)/shard_map/reshape | solution.py:21
  93.9 22.9 %fusion = f32[4096,8,128]{0,2,1:T(8,128)} fusion(f32[4096,8,128]{2,0,1:T(8,128)} %copy.18, f32[8,128]{1,0:T(8,128)S(1)} %convert_bitcast_fusion), kind=kOutput, calls=%fused_computation | convolution fusion | flops 6447235072 | bytes 33558528 | tf_op jit(solution)/shard_map/rbk,kj->rbj/dot_general | solution.py:22
  116.9 0.0 reduce-scatter.2.cloned.1.call-update
  116.9 31.9 %all-gather.3.cloned.1.call-done = bf16[4096,1024]{1,0:T(8,128)(2,1)} async-done(((bf16[512,1024]{1,0:T(8,128)(2,1)}), bf16[4096,1024]{1,0:T(8,128)(2,1)}) %all-gather.3.cloned.1.call-update) | async-done | bytes 8388624 | tf_op jit(solution)/shard_map/all_gather | solution.py:46
  148.8 9.6 %fusion.5 = f32[512,1024]{0,1:T(8,128)S(1)} fusion(bf16[512,4096]{1,0:T(8,128)(2,1)} %all-gather.5.cloned.1.call-done, bf16[4096,1024]{1,0:T(8,128)(2,1)} %all-gather.3.cloned.1.call-done, bf16[4096,1024]{1,0:T(8,128)(2,1)} %param.10), kind=kOutput, calls=%fused_computation.10 | convolution fusion | flops 4311744512 | bytes 23068672 | tf_op jit(solution)/shard_map/dot_general | solution.py:49
  158.5 1.8 copy.23
  160.3 157.6 %reduce-scatter.2.cloned.1.call-done = f32[512,1024]{0,1:T(8,128)} async-done(((f32[4096,1024]{0,1:T(8,128)}), f32[512,1024]{0,1:T(8,128)}) %reduce-scatter.2.cloned.1.call-update) | async-done | bytes 2097168 | tf_op jit(solution)/shard_map/reduce_scatter | solution.py:52
  317.9 5.2 %convolution_multiply_fusion = f32[512,8,128]{0,2,1:T(8,128)} fusion(f32[512,8,128]{0,2,1:T(8,128)} %bitcast.19, f32[8,128]{1,0:T(8,128)S(1)} %convert_bitcast_fusion), kind=kOutput, calls=%fused_computation.11 | convolution fusion | flops 806420480 | bytes 4198400 | tf_op jit(solution)/shard_map/rbj,jk->rbk/dot_general | solution.py:29
  323.1 1.9 copy.20
  325.0 0.0 copy-start.2
  325.0 0.0 copy-start.1
  325.0 6.9 %multiply_subtract_fusion = (f32[512,1024]{1,0:T(8,128)}, f32[512,1024]{1,0:T(8,128)}, f32[512,1024]{1,0:T(8,128)}) fusion(f32[512,1024]{1,0:T(8,128)} %param.13, f32[512,1024]{1,0:T(8,128)S(1)} %copy.20, f32[512,1024]{1,0:T(8,128)} %param.14, f32[512,1024]{1,0:T(8,128)} %param.15), kind=kLoop, calls=%fused_computation.8 | loop fusion | flops 7864320 | bytes 14680064 | tf_op jit(solution)/shard_map/sub | solution.py:61
  331.9 0.0 copy-done.2
  331.9 0.9 abs_reduce_fusion
  332.8 0.0 copy-done.1
  (1 shorter events, 0.0 us)
Async XLA Ops:
  7.2 58.0 %copy-start = (bf16[512,1024]{1,0:T(8,128)(2,1)S(1)}, bf16[512,1024]{1,0:T(8,128)(2,1)}, u32[]{:S(2)}) copy-start(bf16[512,1024]{1,0:T(8,128)(2,1)} %param.9) | copy-start | bytes 3145732
  7.2 1.5 copy-start.3
  7.2 58.0 %all-gather.5.cloned.1.call-start = ((), (), s32[]{:S(2)}) async-start(), calls=%async_computation.2 | async-start | bytes 5242880 | tf_op jit(solution)/shard_map/all_gather | solution.py:43
  7.9 140.9 %all-gather.3.cloned.1.call-start = ((), (), s32[]{:S(2)}) async-start(), calls=%async_computation.1 | async-start | bytes 9437184 | tf_op jit(solution)/shard_map/all_gather | solution.py:46
  8.7 309.2 %reduce-scatter.2.cloned.1.call-start = ((), (), s32[]{:S(2)}) async-start(), calls=%async_computation.3 | async-start | bytes 18874368 | tf_op jit(solution)/shard_map/reduce_scatter | solution.py:52
  325.0 6.9 %copy-start.2 = (f32[512,1024]{0,1:T(8,128)S(1)}, f32[512,1024]{0,1:T(8,128)}, u32[]{:S(2)}) copy-start(f32[512,1024]{0,1:T(8,128)} %reduce-scatter.2.cloned.1.call-done) | copy-start | bytes 6291460
  325.0 7.8 %copy-start.1 = (bf16[512,1024]{1,0:T(8,128)(2,1)S(1)}, bf16[512,1024]{1,0:T(8,128)(2,1)}, u32[]{:S(2)}) copy-start(bf16[512,1024]{1,0:T(8,128)(2,1)} %param.9) | copy-start | bytes 3145732
Sparse Core Ops, SparseCore 0:
  9.8 55.2 all-gather.4
  66.8 82.0 all-gather.2
  151.2 166.6 reduce-scatter.1
where the time goes:
time: 340 us; the launch traced here: 339 us
  waiting for transfers between devices  247 us (73%)
  matrix products  48.7 us (14%)
  local copies, waits for them, and re-layouts  21.5 us (6%)
  between operations  13.8 us (4%)
  other arithmetic  7.74 us (2%)
    reduce_scatter x1, waiting for transfers between devices, body(): lax.psum_scatter(smooth(partial_value, signs, table), 'inner', scatter_di...  158 us
    all_gather x1, waiting for transfers between devices, body(): gathered = lax.all_gather(tokens, 'outer', axis=1, tiled=True)  56.4 us
    all_gather x1, waiting for transfers between devices, body(): lax.all_gather(weight_delta, 'inner', axis=0, tiled=True)  31.9 us
    dot_general x1, matrix products, smooth(): jnp.einsum('rbk,kj->rbj', blocks, table, precision=lax.Precision.HIGHEST)  22.9 us
    reshape x1, local copies, waits for them, and re-layouts, smooth(): values.reshape(height, -1, table.shape[0])  17.8 us
    dot_general x1, matrix products, outer_product(): lax.dot_general(left, right, (((0,), (0,)), ((), ())), preferred_element_...  11 us
    dot_general x1, matrix products, body(): output = jnp.dot(columns, merged, preferred_element_type=jnp.float32)  9.64 us
    sub x1, other arithmetic, body(): new_master = master - 0.01 * (corrected / spread + 0.1 * master)  6.87 us
  transfers between devices with their start and end apart: 3, of which 3 were waited for; matrix products, arithmetic and copies ran while one was open for 19% of the time, Pallas kernels for 0%

commit v1 on v0

--- a/solution.py
+++ b/solution.py
@@ -4,6 +4,19 @@
 from jax.sharding import PartitionSpec as P
 
 BLOCK = 128
+
+
+def ring_gather(x, axis, dim):
+    size, mine, rows = (lax.axis_size(axis), lax.axis_index(axis), x.shape[dim])
+    ahead = [(i, (i + 1) % size) for i in range(size)]
+    filled = jnp.zeros((*x.shape[:dim], size * rows, *x.shape[dim + 1 :]), x.dtype)
+    block = x
+    for step in range(size):
+        holder = (mine - step) % size
+        filled = lax.dynamic_update_slice_in_dim(filled, block, holder * rows, axis=dim)
+        if step < size - 1:
+            block = lax.ppermute(block, axis, ahead)
+    return filled
 
 
 def hadamard_table(length):
@@ -42,8 +55,7 @@
     shard_rows = master.shape[0]
     gathered = lax.all_gather(tokens, "outer", axis=1, tiled=True)
     merged = (
-        weight_cache.astype(jnp.float32)
-        + lax.all_gather(weight_delta, "inner", axis=0, tiled=True).astype(jnp.float32)
+        weight_cache.astype(jnp.float32) + ring_gather(weight_delta, "inner", 0).astype(jnp.float32)
     ).astype(jnp.bfloat16)
     columns = gathered
     output = jnp.dot(columns, merged, preferred_element_type=jnp.float32)

time: 340 us -> 392 us (1.15)
  waiting for transfers between devices: 247 us -> 292 us
  local copies, waits for them, and re-layouts: 21.5 us -> 31.1 us
    ppermute x0 -> x7, waiting for transfers between devices: none -> 235 us  [ring_gather(): block = lax.ppermute(block, axis, ahead)]
    reduce_scatter x1, waiting for transfers between devices: 158 us -> 0.01 us  [body(): lax.psum_scatter(smooth(partial_value, signs, table), 'inner', scatter_di...]
    all_gather x1 -> x0, waiting for transfers between devices: 31.9 us -> none  [body(): lax.all_gather(weight_delta, 'inner', axis=0, tiled=True)]
    unnamed x9 -> x23, local copies, waits for them, and re-layouts: 1.84 us -> 7.26 us
  transfers between devices with their start and end apart: 3 -> 9, of which waited for: 3 -> 8; matrix products, arithmetic and copies ran while one was open for 19% -> 4% of each run, Pallas kernels for 0% -> 0%
where the time goes in v1:
time: 392 us
  waiting for transfers between devices  292 us (74%)
  matrix products  45.4 us (12%)
  local copies, waits for them, and re-layouts  31.1 us (8%)
  between operations  14.2 us (4%)
  other arithmetic  8.43 us (2%)
    ppermute x7, waiting for transfers between devices, ring_gather(): block = lax.ppermute(block, axis, ahead)  235 us
    all_gather x1, waiting for transfers between devices, body(): gathered = lax.all_gather(tokens, 'outer', axis=1, tiled=True)  56.5 us
    dot_general x1, matrix products, smooth(): jnp.einsum('rbk,kj->rbj', blocks, table, precision=lax.Precision.HIGHEST)  22.8 us
    reshape x1, local copies, waits for them, and re-layouts, smooth(): values.reshape(height, -1, table.shape[0])  17.4 us
    dot_general x1, matrix products, outer_product(): lax.dot_general(left, right, (((0,), (0,)), ((), ())), preferred_element_...  10.3 us
  transfers between devices with their start and end apart: 9, of which 8 were waited for; matrix products, arithmetic and copies ran while one was open for 4% of the time, Pallas kernels for 0%

profile of v1, /device:TPU:0, one launch (start us, length us, event | category | flops | bytes accessed | tf_op | source)
XLA Modules:
  0.0 391.7 jit_solution(10975659063127363210)
XLA Ops:
  7.2 0.0 copy-start
  7.2 0.0 all-gather.2.cloned.1.call-start
  7.2 0.7 all-gather.2.cloned.1.call-update
  7.9 0.0 reduce-scatter.2.cloned.1.call-start
  8.0 0.7 convert_bitcast_fusion
  8.7 56.5 %all-gather.2.cloned.1.call-done = bf16[512,4096]{1,0:T(8,128)(2,1)} async-done(((bf16[512,1024]{1,0:T(8,128)(2,1)}), bf16[512,4096]{1,0:T(8,128)(2,1)}) %all-gather.2.cloned.1.call-update) | async-done | bytes 4194320 | tf_op jit(solution)/shard_map/all_gather | solution.py:56
  65.2 0.0 copy-done
  65.2 10.3 %fusion.47 = f32[4096,1024]{0,1:T(8,128)} fusion(bf16[512,4096]{1,0:T(8,128)(2,1)} %all-gather.2.cloned.1.call-done, bf16[512,1024]{1,0:T(8,128)(2,1)S(1)} %copy-done), kind=kOutput, calls=%fused_computation.62 | convolution fusion | flops 4294967296 | bytes 22020096 | tf_op jit(solution)/shard_map/dot_general | solution.py:47
  75.5 17.4 %copy.18 = f32[4096,8,128]{2,0,1:T(8,128)} copy(f32[4096,8,128]{0,2,1:T(8,128)} %bitcast.18) | data formatting | bytes 33554432 | tf_op jit(solution)/shard_map/reshape | solution.py:34
  92.9 22.8 %fusion = f32[4096,8,128]{0,2,1:T(8,128)} fusion(f32[4096,8,128]{2,0,1:T(8,128)} %copy.18, f32[8,128]{1,0:T(8,128)S(1)} %convert_bitcast_fusion), kind=kOutput, calls=%fused_computation | convolution fusion | flops 6447235072 | bytes 33558528 | tf_op jit(solution)/shard_map/rbk,kj->rbj/dot_general | solution.py:35
  115.7 0.0 copy-start.3
  115.7 0.0 reduce-scatter.2.cloned.1.call-update
  115.7 1.2 copy-done.3
  116.9 0.0 collective-permute-start
  116.9 30.4 %collective-permute-done = bf16[512,1024]{1,0:T(8,128)(2,1)S(1)} collective-permute-done((bf16[512,1024]{1,0:T(8,128)(2,1)S(1)}, bf16[512,1024]{1,0:T(8,128)(2,1)S(1)}, u32[]{:S(2)}, u32[]{:S(2)}) %collective-permute-start) | collective-permute-done | bytes 1048608 | tf_op jit(solution)/shard_map/ppermute | solution.py:18
  147.3 0.0 collective-permute-start.1
  147.3 38.6 %collective-permute-done.1 = bf16[512,1024]{1,0:T(8,128)(2,1)S(1)} collective-permute-done((bf16[512,1024]{1,0:T(8,128)(2,1)S(1)}, bf16[512,1024]{1,0:T(8,128)(2,1)S(1)}, u32[]{:S(2)}, u32[]{:S(2)}) %collective-permute-start.1) | collective-permute-done | bytes 1048608 | tf_op jit(solution)/shard_map/ppermute | solution.py:18
  185.9 0.0 collective-permute-start.2
  185.9 38.6 %collective-permute-done.2 = bf16[512,1024]{1,0:T(8,128)(2,1)S(1)} collective-permute-done((bf16[512,1024]{1,0:T(8,128)(2,1)S(1)}, bf16[512,1024]{1,0:T(8,128)(2,1)S(1)}, u32[]{:S(2)}, u32[]{:S(2)}) %collective-permute-start.2) | collective-permute-done | bytes 1048608 | tf_op jit(solution)/shard_map/ppermute | solution.py:18
  224.5 0.0 copy-start.4
  224.5 1.0 copy-done.4
  225.5 0.0 collective-permute-start.3
  225.5 38.6 %collective-permute-done.3 = bf16[512,1024]{1,0:T(8,128)(2,1)S(1)} collective-permute-done((bf16[512,1024]{1,0:T(8,128)(2,1)S(1)}, bf16[512,1024]{1,0:T(8,128)(2,1)S(1)}, u32[]{:S(2)}, u32[]{:S(2)}) %collective-permute-start.3) | collective-permute-done | bytes 1048608 | tf_op jit(solution)/shard_map/ppermute | solution.py:18
  264.1 0.0 copy-start.6
  264.1 1.0 copy-done.6
  265.1 0.0 collective-permute-start.4
  265.1 38.6 %collective-permute-done.4 = bf16[512,1024]{1,0:T(8,128)(2,1)S(1)} collective-permute-done((bf16[512,1024]{1,0:T(8,128)(2,1)S(1)}, bf16[512,1024]{1,0:T(8,128)(2,1)S(1)}, u32[]{:S(2)}, u32[]{:S(2)}) %collective-permute-start.4) | collective-permute-done | bytes 1048608 | tf_op jit(solution)/shard_map/ppermute | solution.py:18
  303.7 0.0 copy-start.8
  303.7 1.0 copy-done.8
  304.6 0.0 collective-permute-start.5
  304.6 38.7 %collective-permute-done.5 = bf16[512,1024]{1,0:T(8,128)(2,1)} collective-permute-done((bf16[512,1024]{1,0:T(8,128)(2,1)S(1)}, bf16[512,1024]{1,0:T(8,128)(2,1)}, u32[]{:S(2)}, u32[]{:S(2)}) %collective-permute-start.5) | collective-permute-done | bytes 1048608 | tf_op jit(solution)/shard_map/ppermute | solution.py:18
  343.4 0.0 collective-permute-start.6
  343.4 1.1 broadcast_in_dim.2
  344.4 0.0 copy-start.5
  344.5 0.0 copy-start.7
  344.5 0.1 constant_dynamic-update-slice_fusion.7
  344.6 0.0 copy-start.9
  344.6 0.1 constant_dynamic-update-slice_fusion.6
  344.7 0.1 constant_dynamic-update-slice_fusion.5
  344.8 0.9 copy-done.5
  345.7 0.1 constant_dynamic-update-slice_fusion.4
  345.8 0.2 copy-done.7
  346.0 0.1 constant_dynamic-update-slice_fusion.3
  346.1 0.2 copy-done.9
  346.4 0.0 copy-start.10
  346.4 0.1 constant_dynamic-update-slice_fusion.2
  346.5 1.5 constant_dynamic-update-slice_fusion.1
  348.0 11.7 %collective-permute-done.6 = bf16[512,1024]{1,0:T(8,128)(2,1)} collective-permute-done((bf16[512,1024]{1,0:T(8,128)(2,1)}, bf16[512,1024]{1,0:T(8,128)(2,1)}, u32[]{:S(2)}, u32[]{:S(2)}) %collective-permute-start.6) | collective-permute-done | bytes 1048608 | tf_op jit(solution)/shard_map/ppermute | solution.py:18
  359.7 1.3 constant_dynamic-update-slice_fusion
  361.0 0.0 copy-done.10
  361.0 7.1 %fusion.5 = f32[512,1024]{0,1:T(8,128)S(1)} fusion(bf16[512,4096]{1,0:T(8,128)(2,1)S(1)} %copy-done.10, bf16[4096,1024]{1,0:T(8,128)(2,1)S(1)} %constant_dynamic-update-slice_fusion, bf16[4096,1024]{1,0:T(8,128)(2,1)} %param.10), kind=kOutput, calls=%fused_computation.10 | convolution fusion | flops 4311744512 | bytes 23068672 | tf_op jit(solution)/shard_map/dot_general | solution.py:61
  368.2 1.8 copy.23
  370.0 0.0 reduce-scatter.2.cloned.1.call-done
  370.0 5.2 %convolution_multiply_fusion = f32[512,8,128]{0,2,1:T(8,128)} fusion(f32[512,8,128]{0,2,1:T(8,128)} %bitcast.19, f32[8,128]{1,0:T(8,128)S(1)} %convert_bitcast_fusion), kind=kOutput, calls=%fused_computation.11 | convolution fusion | flops 806420480 | bytes 4198400 | tf_op jit(solution)/shard_map/rbj,jk->rbk/dot_general | solution.py:42
  375.2 1.9 copy.20
  377.1 0.0 copy-start.2
  377.1 0.0 copy-start.1
  377.1 6.9 %multiply_subtract_fusion = (f32[512,1024]{1,0:T(8,128)}, f32[512,1024]{1,0:T(8,128)}, f32[512,1024]{1,0:T(8,128)}) fusion(f32[512,1024]{1,0:T(8,128)} %param.13, f32[512,1024]{1,0:T(8,128)S(1)} %copy.20, f32[512,1024]{1,0:T(8,128)} %param.14, f32[512,1024]{1,0:T(8,128)} %param.15), kind=kLoop, calls=%fused_computation.8 | loop fusion | flops 7864320 | bytes 14680064 | tf_op jit(solution)/shard_map/sub | solution.py:73
  384.0 0.0 copy-done.2
  384.0 0.9 abs_reduce_fusion
  384.9 0.0 copy-done.1
Async XLA Ops:
  7.2 58.0 %copy-start = (bf16[512,1024]{1,0:T(8,128)(2,1)S(1)}, bf16[512,1024]{1,0:T(8,128)(2,1)}, u32[]{:S(2)}) copy-start(bf16[512,1024]{1,0:T(8,128)(2,1)} %param.9) | copy-start | bytes 3145732
  7.2 58.0 %all-gather.2.cloned.1.call-start = ((), (), s32[]{:S(2)}) async-start(), calls=%async_computation.1 | async-start | bytes 5242880 | tf_op jit(solution)/shard_map/all_gather | solution.py:56
  7.9 362.1 %reduce-scatter.2.cloned.1.call-start = ((), (), s32[]{:S(2)}) async-start(), calls=%async_computation.2 | async-start | bytes 18874368 | tf_op jit(solution)/shard_map/reduce_scatter | solution.py:64
  115.7 1.2 copy-start.3
  116.9 30.4 %collective-permute-start = (bf16[512,1024]{1,0:T(8,128)(2,1)S(1)}, bf16[512,1024]{1,0:T(8,128)(2,1)S(1)}, u32[]{:S(2)}, u32[]{:S(2)}) collective-permute-start(bf16[512,1024]{1,0:T(8,128)(2,1)S(1)} %copy-done.3), channel_id=1, source_target_pairs={{0,1},{1,2},{2,3},{3,4},{4,5},{5,6},{6,7},{7,0},{8,9},{9,10},{10,1... | collective-permute-start | bytes 3145736 | tf_op jit(solution)/shard_map/ppermute | solution.py:18
  147.3 38.6 %collective-permute-start.1 = (bf16[512,1024]{1,0:T(8,128)(2,1)S(1)}, bf16[512,1024]{1,0:T(8,128)(2,1)S(1)}, u32[]{:S(2)}, u32[]{:S(2)}) collective-permute-start(bf16[512,1024]{1,0:T(8,128)(2,1)S(1)} %collective-permute-done), channel_id=1, source_target_pairs={{0,1},{1,2},{2,3},{3,4},{4,5},{5,6},{6,7},{7,0},{8,9},{9,10},{10,1... | collective-permute-start | bytes 3145736 | tf_op jit(solution)/shard_map/ppermute | solution.py:18
  185.9 38.6 %collective-permute-start.2 = (bf16[512,1024]{1,0:T(8,128)(2,1)S(1)}, bf16[512,1024]{1,0:T(8,128)(2,1)S(1)}, u32[]{:S(2)}, u32[]{:S(2)}) collective-permute-start(bf16[512,1024]{1,0:T(8,128)(2,1)S(1)} %collective-permute-done.1), channel_id=1, source_target_pairs={{0,1},{1,2},{2,3},{3,4},{4,5},{5,6},{6,7},{7,0},{8,9},{9,10},{10,1... | collective-permute-start | bytes 3145736 | tf_op jit(solution)/shard_map/ppermute | solution.py:18
  224.5 1.0 copy-start.4
  225.5 38.6 %collective-permute-start.3 = (bf16[512,1024]{1,0:T(8,128)(2,1)S(1)}, bf16[512,1024]{1,0:T(8,128)(2,1)S(1)}, u32[]{:S(2)}, u32[]{:S(2)}) collective-permute-start(bf16[512,1024]{1,0:T(8,128)(2,1)S(1)} %collective-permute-done.2), channel_id=1, source_target_pairs={{0,1},{1,2},{2,3},{3,4},{4,5},{5,6},{6,7},{7,0},{8,9},{9,10},{10,1... | collective-permute-start | bytes 3145736 | tf_op jit(solution)/shard_map/ppermute | solution.py:18
  264.1 1.0 copy-start.6
  265.1 38.6 %collective-permute-start.4 = (bf16[512,1024]{1,0:T(8,128)(2,1)S(1)}, bf16[512,1024]{1,0:T(8,128)(2,1)S(1)}, u32[]{:S(2)}, u32[]{:S(2)}) collective-permute-start(bf16[512,1024]{1,0:T(8,128)(2,1)S(1)} %collective-permute-done.3), channel_id=1, source_target_pairs={{0,1},{1,2},{2,3},{3,4},{4,5},{5,6},{6,7},{7,0},{8,9},{9,10},{10,1... | collective-permute-start | bytes 3145736 | tf_op jit(solution)/shard_map/ppermute | solution.py:18
  303.7 1.0 copy-start.8
  304.6 38.7 %collective-permute-start.5 = (bf16[512,1024]{1,0:T(8,128)(2,1)S(1)}, bf16[512,1024]{1,0:T(8,128)(2,1)}, u32[]{:S(2)}, u32[]{:S(2)}) collective-permute-start(bf16[512,1024]{1,0:T(8,128)(2,1)S(1)} %collective-permute-done.4), channel_id=1, source_target_pairs={{0,1},{1,2},{2,3},{3,4},{4,5},{5,6},{6,7},{7,0},{8,9},{9,10},{10,1... | collective-permute-start | bytes 3145736 | tf_op jit(solution)/shard_map/ppermute | solution.py:18
  343.4 16.3 %collective-permute-start.6 = (bf16[512,1024]{1,0:T(8,128)(2,1)}, bf16[512,1024]{1,0:T(8,128)(2,1)}, u32[]{:S(2)}, u32[]{:S(2)}) collective-permute-start(bf16[512,1024]{1,0:T(8,128)(2,1)} %collective-permute-done.5), channel_id=1, source_target_pairs={{0,1},{1,2},{2,3},{3,4},{4,5},{5,6},{6,7},{7,0},{8,9},{9,10},{10,1... | collective-permute-start | bytes 3145736 | tf_op jit(solution)/shard_map/ppermute | solution.py:18
  344.4 1.3 copy-start.5
  344.5 1.6 copy-start.7
  344.6 1.8 copy-start.9
  346.4 14.7 %copy-start.10 = (bf16[512,4096]{1,0:T(8,128)(2,1)S(1)}, bf16[512,4096]{1,0:T(8,128)(2,1)}, u32[]{:S(2)}) copy-start(bf16[512,4096]{1,0:T(8,128)(2,1)} %all-gather.2.cloned.1.call-done) | copy-start | bytes 12582916
  377.1 6.9 %copy-start.2 = (f32[512,1024]{0,1:T(8,128)S(1)}, f32[512,1024]{0,1:T(8,128)}, u32[]{:S(2)}) copy-start(f32[512,1024]{0,1:T(8,128)} %reduce-scatter.2.cloned.1.call-done) | copy-start | bytes 6291460
  377.1 7.8 %copy-start.1 = (bf16[512,1024]{1,0:T(8,128)(2,1)S(1)}, bf16[512,1024]{1,0:T(8,128)(2,1)}, u32[]{:S(2)}) copy-start(bf16[512,1024]{1,0:T(8,128)(2,1)} %param.9) | copy-start | bytes 3145732
Sparse Core Ops, SparseCore 0:
  9.8 55.2 all-gather.1
  115.8 232.2 reduce-scatter.1
